TPU v7x, 256 devices: a whole 4x4x8 slice. The times are simulated.
256 devices in a mesh: blk: 32 (over y_lo, z, core), col: 8 (over y_hi, x).
Axes of the slice: x: 4, y: 4 (y_hi: 2, y_lo: 2; y = y_hi * 2 + y_lo), z: 8, core: 2. Of those that a mesh axis runs over, the one named last changes fastest.
Arguments:
- counts: float32 [8192, 8192], P('blk', 'col'), may hold values from 0.1 to 10
- merge_map: int32 [8192, 1], replicated, may hold values from 0 to 4095, as said below
Outputs:
- merged: float32 [4096, 4096], P('blk', 'col')
- block_terms: float32 [4096], P('blk')
Inputs may be any that keep to these rules, and one draw needn't show every extreme that they name: `merge_map`: every new block is the image of exactly two old blocks. Let the owner of new block r be r // 128. The 256 old blocks i with i // 256 = s, for each s, map to new blocks of exactly 16 distinct owners, exactly 16 old blocks to each of them, and each owner receives from exactly 16 such s.
All inputs are finite; a program needn't handle non-finite values.
Results may differ from a plain program's by a relative error of at most 0.0003.
Values sent between devices are 32-bit elements; how exact they have to be, the bound alone decides.
A program may use at most 64 MiB of HBM per device.

v0:
```python
import jax
import jax.numpy as jnp
from jax import lax
from jax.sharding import PartitionSpec as P

NB = 4096


HIGH = lax.Precision.HIGHEST


def cut_along(x, dim, devices):
    shape = x.shape
    blocks = x.reshape(*shape[:dim], devices, shape[dim] // devices, *shape[dim + 1 :])
    return jnp.moveaxis(blocks, dim, 0)


def sent_and_summed(x, axis, dim):
    blocks = cut_along(x, dim, lax.axis_size(axis))
    arrived = lax.all_to_all(blocks, axis, split_axis=0, concat_axis=0, tiled=True)
    return arrived.sum(axis=0)


def sent_to_all(x, axis):
    devices = lax.axis_size(axis)
    return lax.all_to_all(jnp.broadcast_to(x[None], (devices, *x.shape)), axis, 0, 0, tiled=True)


def of_everyone(x, axis):
    everything = sent_to_all(x, axis)
    return jnp.sum(everything, axis=0)


def in_one(arrays, axis):
    ends = [0]
    for a in arrays:
        ends.append(ends[-1] + a.size)
    so_far = of_everyone(jnp.concatenate([a.ravel() for a in arrays]), axis)
    return tuple((so_far[b:e].reshape(a.shape) for a, b, e in zip(arrays, ends, ends[1:])))


def one_hot_block(labels, count):
    targets = jnp.arange(count, dtype=jnp.int32)
    return (labels[:, None] == targets[None, :]).astype(jnp.float32)


def pack_rows(matrix, labels, owned, groups, capacity):
    width = matrix.shape[1]
    owner = labels // owned
    table = (owner[:, None] == jnp.arange(groups, dtype=jnp.int32)[None, :]).astype(jnp.int32)
    ranks = jnp.sum(jnp.cumsum(table, axis=0) * table, axis=1) - 1
    target = owner * capacity + ranks
    buffer = jnp.zeros((groups * capacity, width), jnp.float32).at[target].set(matrix)
    tags = jnp.full((groups * capacity,), -1, jnp.int32).at[target].set(labels)
    return (buffer.reshape(groups, capacity, width), tags.reshape(groups, capacity))


def unpack_rows(buffer, tags, owned):
    width = buffer.shape[2]
    local_ids = tags.reshape(-1) - lax.axis_index("blk") * owned
    table = one_hot_block(local_ids, owned)
    flat = buffer.reshape(-1, width)
    return lax.dot_general(
        table, flat, (((0,), (0,)), ((), ())), precision=HIGH, preferred_element_type=jnp.float32
    )


def shards(counts, merge_map):
    row_len = counts.shape[0]
    col_len = counts.shape[1]
    groups = lax.axis_size("blk")
    columns_axis = lax.axis_size("col")
    owned = NB // groups
    owned_cols = NB // columns_axis
    fanout = min(groups // 2, row_len // 2)
    capacity = row_len // fanout
    ids = merge_map[:, 0]
    row_labels = lax.dynamic_slice_in_dim(ids, lax.axis_index("blk") * row_len, row_len, 0)
    col_labels = lax.dynamic_slice_in_dim(ids, lax.axis_index("col") * col_len, col_len, 0)
    buffer, tags = pack_rows(counts, row_labels, owned, groups, capacity)
    got_rows, got_tags = (
        lax.all_to_all(buffer, "blk", split_axis=0, concat_axis=0, tiled=True),
        lax.all_to_all(tags, "blk", split_axis=0, concat_axis=0, tiled=True),
    )
    row_merged = unpack_rows(got_rows, got_tags, owned)
    table = one_hot_block(col_labels, owned_cols * lax.axis_size("col"))
    merged = sent_and_summed(
        lax.dot_general(
            table,
            row_merged,
            (((0,), (1,)), ((), ())),
            precision=HIGH,
            preferred_element_type=jnp.float32,
        ),
        "col",
        0,
    ).T
    in_total = of_everyone(jnp.sum(merged, axis=0), "blk")
    out_total, total = in_one((jnp.sum(merged, axis=1), jnp.sum(in_total)), "col")
    share = merged / out_total[:, None]
    ratio = merged * total / (out_total[:, None] * in_total[None, :])
    partial_terms = jnp.sum(share * jnp.log(ratio), axis=1)
    block_terms = of_everyone(partial_terms, "col")
    return (merged, block_terms)


def solution(mesh):
    placed = (P("blk", "col"), P())
    return jax.shard_map(
        shards, mesh=mesh, in_specs=placed, out_specs=(P("blk", "col"), P("blk")), check_vma=False
    )
```

profile of v0, /device:TPU:1, one launch (start us, length us, event | category | flops | bytes accessed | tf_op | source)
XLA Modules:
  0.0 159.6 jit_solution(10830408640562494884)
XLA Ops:
  0.6 0.7 and_select_fusion
  1.3 0.6 reduce-window.6
  2.3 1.4 scatter_custom_fusion
  3.7 0.7 all_to_all.24
  4.4 11.1 %all-to-all-start = ((s32[32,1,16]{2,1,0:T(1,128)}), s32[32,1,16]{2,1,0:T(1,128)S(1)}, u32[]{:S(2)}, u32[]{:S(2)}) async-start(s32[32,1,16]{2,1,0:T(1,128)} %bitcast.7), calls=%async_computation | async-start | bytes 32768 | tf_op jit(solution)/shard_map/all_to_all | solution.py:83
  15.5 3.5 %scatter_custom_fusion.1 = f32[512,1024]{1,0:T(8,128)} fusion(s32[256]{0:T(256)S(1)} %bitcast.42, f32[256,1024]{1,0:T(8,128)} %param.2, f32[]{:T(128)} %constant.49.clone.1), kind=kCustom, calls=%fused_computation.6 | custom fusion | bytes 2097664 | tf_op jit(solution)/shard_map/scatter | solution.py:53
  19.1 4.2 %all-to-all-done = s32[32,1,16]{2,1,0:T(1,128)S(1)} async-done(((s32[32,1,16]{2,1,0:T(1,128)}), s32[32,1,16]{2,1,0:T(1,128)S(1)}, u32[]{:S(2)}, u32[]{:S(2)}) %all-to-all-start) | async-done | bytes 2080 | tf_op jit(solution)/shard_map/all_to_all | solution.py:83
  23.3 4.5 %all-to-all-start.1 = ((f32[32,16,1024]{2,1,0:T(8,128)}), f32[32,16,1024]{2,1,0:T(8,128)S(1)}, u32[]{:S(2)}, u32[]{:S(2)}) async-start(f32[32,16,1024]{2,1,0:T(8,128)} %bitcast.8), calls=%async_computation.1 | async-start | bytes 4194304 | tf_op jit(solution)/shard_map/all_to_all | solution.py:82
  27.8 0.7 constant_dynamic-slice_fusion.1
  28.6 48.5 %all-to-all-done.1 = f32[32,16,1024]{2,1,0:T(8,128)S(1)} async-done(((f32[32,16,1024]{2,1,0:T(8,128)}), f32[32,16,1024]{2,1,0:T(8,128)S(1)}, u32[]{:S(2)}, u32[]{:S(2)}) %all-to-all-start.1) | async-done | bytes 2097184 | tf_op jit(solution)/shard_map/all_to_all | solution.py:82
  77.1 1.0 fusion.6
  78.1 9.8 %fusion.1 = f32[4096,128]{1,0:T(8,128)S(1)} fusion(f32[128,1024]{1,0:T(8,128)S(1)} %fusion.6, s32[1024]{0:T(1024)S(1)} %bitcast.39), kind=kOutput, calls=%fused_computation.4 | convolution fusion | flops 6450839552 | bytes 2625536 | tf_op jit(solution)/shard_map/dot_general | solution.py:88
  87.9 33.4 %all_to_all.37 = f32[8,512,128]{2,1,0:T(8,128)S(1)} all-to-all(f32[8,512,128]{2,1,0:T(8,128)S(1)} %bitcast.34), channel_id=1, replica_groups=mesh['blk'=32,'col'=8] {'col'}, dimensions={0} | all-to-all | bytes 4194304 | tf_op jit(solution)/shard_map/all_to_all | solution.py:20
  121.3 0.6 fusion.13
  121.9 14.7 %all_to_all.38 = f32[32,1,512]{2,1,0:T(1,128)S(1)} all-to-all(f32[32,1,512]{2,1,0:T(1,128)S(1)} %broadcast_in_dim.12), channel_id=1, replica_groups=mesh['blk'=32,'col'=8] {'blk'}, dimensions={0} | all-to-all | bytes 131072 | tf_op jit(solution)/shard_map/all_to_all | solution.py:26
  136.6 0.7 fusion.14
  137.3 0.7 pad_maximum_fusion
  138.0 9.3 %all_to_all.39 = f32[8,1,129]{2,1,0:T(1,128)S(1)} all-to-all(f32[8,1,129]{2,1,0:T(1,128)S(1)} %broadcast_in_dim.13), channel_id=1, replica_groups=mesh['blk'=32,'col'=8] {'col'}, dimensions={0} | all-to-all | bytes 8256 | tf_op jit(solution)/shard_map/all_to_all | solution.py:26
  147.8 0.8 multiply_reduce_fusion
  148.6 0.6 broadcast_in_dim.14
  149.3 3.3 %all-to-all-start.5 = ((f32[8,1,128]{2,1,0:T(1,128)}), f32[8,1,128]{2,1,0:T(1,128)S(1)}, u32[]{:S(2)}, u32[]{:S(2)}) async-start(f32[8,1,128]{2,1,0:T(1,128)} %broadcast_in_dim.14), calls=%async_computation.5 | async-start | bytes 8192 | tf_op jit(solution)/shard_map/all_to_all | solution.py:26
  152.6 0.8 copy.17
  153.4 5.6 %all-to-all-done.5 = f32[8,1,128]{2,1,0:T(1,128)S(1)} async-done(((f32[8,1,128]{2,1,0:T(1,128)}), f32[8,1,128]{2,1,0:T(1,128)S(1)}, u32[]{:S(2)}, u32[]{:S(2)}) %all-to-all-start.5) | async-done | bytes 4128 | tf_op jit(solution)/shard_map/all_to_all | solution.py:26
  159.1 0.5 reduce_sum.89
  (14 shorter events, 1.1 us)
Async XLA Ops:
  4.4 18.9 %all-to-all-start = ((s32[32,1,16]{2,1,0:T(1,128)}), s32[32,1,16]{2,1,0:T(1,128)S(1)}, u32[]{:S(2)}, u32[]{:S(2)}) async-start(s32[32,1,16]{2,1,0:T(1,128)} %bitcast.7), calls=%async_computation | async-start | bytes 32768 | tf_op jit(solution)/shard_map/all_to_all | solution.py:83
  23.3 53.8 %all-to-all-start.1 = ((f32[32,16,1024]{2,1,0:T(8,128)}), f32[32,16,1024]{2,1,0:T(8,128)S(1)}, u32[]{:S(2)}, u32[]{:S(2)}) async-start(f32[32,16,1024]{2,1,0:T(8,128)} %bitcast.8), calls=%async_computation.1 | async-start | bytes 4194304 | tf_op jit(solution)/shard_map/all_to_all | solution.py:82
  149.3 9.8 %all-to-all-start.5 = ((f32[8,1,128]{2,1,0:T(1,128)}), f32[8,1,128]{2,1,0:T(1,128)S(1)}, u32[]{:S(2)}, u32[]{:S(2)}) async-start(f32[8,1,128]{2,1,0:T(1,128)} %broadcast_in_dim.14), calls=%async_computation.5 | async-start | bytes 8192 | tf_op jit(solution)/shard_map/all_to_all | solution.py:26
where the time goes:
time: 161 us; the launch traced here: 160 us
  waiting for transfers between devices  58.4 us (36%)
  blocking collectives  57.4 us (36%)
  starting transfers between devices  18.9 us (12%)
  matrix products  10.7 us (7%)
  local copies, waits for them, and re-layouts  8.58 us (5%)
  other arithmetic  4.8 us (3%)
    all_to_all x1, waiting for transfers between devices, shards(): lax.all_to_all(buffer, 'blk', split_axis=0, concat_axis=0, tiled=True)  48.5 us
    all_to_all x1, blocking collectives, sent_and_summed(): lax.all_to_all(blocks, axis, split_axis=0, concat_axis=0, tiled=True)  33.4 us
    all_to_all x2, blocking collectives, sent_to_all(): lax.all_to_all(jnp.broadcast_to(x[None], (devices, *x.shape)), axis, 0, 0...  24 us
    all_to_all x1, starting transfers between devices, shards(): lax.all_to_all(tags, 'blk', split_axis=0, concat_axis=0, tiled=True)  11.1 us
    dot_general x1, matrix products, shards(): lax.dot_general(table, row_merged, (((0,), (1,)), ((), ())), precision=HI...  9.77 us
    all_to_all x1, waiting for transfers between devices, sent_to_all(): lax.all_to_all(jnp.broadcast_to(x[None], (devices, *x.shape)), axis, 0, 0...  5.63 us
    all_to_all x1, starting transfers between devices, shards(): lax.all_to_all(buffer, 'blk', split_axis=0, concat_axis=0, tiled=True)  4.48 us
    all_to_all x1, waiting for transfers between devices, shards(): lax.all_to_all(tags, 'blk', split_axis=0, concat_axis=0, tiled=True)  4.23 us
  transfers between devices with their start and end apart: 3, of which 3 were waited for; matrix products, arithmetic and copies ran while one was open for 3% of the time, Pallas kernels for 0%

commit v1 on v0

v1 whole, which is shorter than its diff:
```python
import jax
import jax.numpy as jnp
from jax import lax
from jax.experimental import pallas as pl
from jax.experimental.pallas import tpu as pltpu
from jax.sharding import PartitionSpec as P

MESH = pl.DeviceIdType.MESH
F32 = jnp.float32
BF16 = jnp.bfloat16
I32 = jnp.int32
NQ = 4
NB_PEERS = 31


def split(v):
    high = v.astype(BF16)
    return high, (v - high.astype(F32)).astype(BF16)


def dot_nn(a, b):
    return lax.dot_general(a, b, (((1,), (0,)), ((), ())), preferred_element_type=F32)


def dot_nt(a, b):
    return lax.dot_general(a, b, (((1,), (1,)), ((), ())), preferred_element_type=F32)


def iota(shape, dim):
    return lax.broadcasted_iota(I32, shape, dim)


def one_hot(mask):
    return jnp.where(mask, 1.0, 0.0).astype(BF16)


def slot_keys(rows):
    owners = [lax.shift_right_logical(r, 7) for r in rows]
    hits = [o == iota((32, 256), 0) for o in owners]
    table = jnp.concatenate([jnp.where(h, 1.0, 0.0) for h in hits], axis=0)
    before = one_hot(iota((256, 256), 0) < iota((256, 256), 1))
    counted = dot_nn(table.astype(BF16), before) * table
    ranks = [
        jnp.sum(counted[i * 32 : (i + 1) * 32], axis=0, keepdims=True).astype(I32)
        for i in range(len(rows))
    ]
    return [o * 16 + r for o, r in zip(owners, ranks)]


def kernel(
    counts_hbm,
    ids,
    merged,
    terms,
    counts,
    parts,
    keys,
    coltag,
    rowtag,
    unpack_rows,
    pack_rows,
    mine,
    xsend,
    xrecv,
    ysend,
    yrecv,
    zsend,
    zrecv,
    csend,
    crecv,
    tsend,
    trecv,
    in_sem,
    xs,
    xr,
    ys,
    yr,
    zs,
    zr,
    cs,
    cr,
    ts,
    tr,
):
    b = lax.axis_index("blk")
    c = lax.axis_index("col")
    x = c % 4
    yh = c // 4

    load = pltpu.make_async_copy(counts_hbm, counts, in_sem)
    load.start()

    barrier = pltpu.get_barrier_semaphore()

    def greet(t, carry):
        pl.semaphore_signal(barrier, inc=1, device_id=((b + t) % 32, c), device_id_type=MESH)
        return carry

    lax.fori_loop(1, 32, greet, 0)
    for t in range(1, 8):
        pl.semaphore_signal(barrier, inc=1, device_id=(b, (c + t) % 8), device_id_type=MESH)

    positions = []
    for g, key in enumerate(slot_keys([ids[c * 4 + g] for g in range(4)])):
        owner = lax.shift_right_logical(key, 4)
        to = lax.shift_right_logical(owner, 2)
        dx = (to - x) & 3
        tile = jnp.where(dx == 2, 0, jnp.where(dx == 1, 1, jnp.where(dx == 3, 2, 3)))
        half = (lax.shift_right_logical(to, 2) - yh) & 1
        positions.append((owner & 3) * 512 + tile * 128 + half * 64 + g * 16 + (key & 15))
    position = jnp.concatenate(positions, axis=1)

    load.wait()
    high, low = split(counts[...])
    parts[0] = high
    parts[1] = low
    pl.semaphore_wait(barrier, 38)

    def x_copy(q, dx):
        return pltpu.make_async_remote_copy(
            src_ref=xsend.at[q, dx],
            dst_ref=xrecv.at[q, dx],
            send_sem=xs.at[q, dx],
            recv_sem=xr.at[q, dx],
            device_id=(b, yh * 4 + (x + dx) % 4),
            device_id_type=MESH,
        )

    def pack(q, carry):
        for first, tiles in ((0, (2, 1)), (256, (3, 0))):
            pick = one_hot(position - q * 512 == iota((256, 1024), 0) + first)
            packed = dot_nt(parts[0], pick) + dot_nt(parts[1], pick)
            for i, dx in enumerate(tiles):
                value = packed[:, i * 128 : (i + 1) * 128]
                if dx == 0:
                    xrecv[q, 0] = value
                else:
                    xsend[q, dx] = value
                    x_copy(q, dx).start()
        return carry

    lax.fori_loop(0, NQ, pack, 0)

    def all_keys(i, carry):
        for g, key in enumerate(slot_keys([ids[i * 4 + g] for g in range(4)])):
            keys[i * 4 + g] = key
        return carry

    lax.fori_loop(0, 8, all_keys, 0)

    slot = iota((128, 1), 0)
    half = lax.shift_right_logical(slot, 4) & 1
    wanted = (((half ^ yh) * 4 + x) * 4 + lax.shift_right_logical(slot, 5)) * 16 + (slot & 15)

    def column_tags(i, carry):
        dx, g = i // 4, i % 4
        s = yh * 16 + ((x + 4 - dx) % 4) * 4 + g
        value = (ids[s] & 127) + 1 + half * 128
        tag = jnp.sum(jnp.where(keys[s] == wanted, value, 0).astype(F32), axis=1, keepdims=True)
        for q in range(NQ):
            for p in range(2):
                coltag[q, dx, p, g] = tag[(q * 2 + p) * 16 : (q * 2 + p + 1) * 16]
        return carry

    lax.fori_loop(0, 16, column_tags, 0)

    def row_tags(s, carry):
        value = (ids[s] & 127) + 1
        hit = keys[s] == b * 16 + iota((16, 1), 0)
        rowtag[s] = jnp.sum(jnp.where(hit, value, 0).astype(F32), axis=1, keepdims=True)
        return carry

    lax.fori_loop(0, 32, row_tags, 0)
    flat = rowtag[...].reshape(512, 1).astype(I32)
    unpack_rows[...] = jnp.where(flat == iota((512, 128), 1) + 1, 1.0, 0.0).T.astype(BF16)
    pack_rows[...] = one_hot(keys[b] == iota((512, 256), 0))

    def y_copy(q):
        return pltpu.make_async_remote_copy(
            src_ref=ysend.at[q],
            dst_ref=yrecv.at[q],
            send_sem=ys.at[q],
            recv_sem=yr.at[q],
            device_id=(b, (c + 4) % 8),
            device_id_type=MESH,
        )

    def after_x(q):
        for dx in range(1, 4):
            x_copy(q, dx).wait_recv()
        tag = coltag[q].reshape(512, 1).astype(I32)
        place = one_hot(tag == iota((512, 256), 1) + 1)
        got = jnp.concatenate([xrecv[q, dx] for dx in range(4)], axis=1)
        high, low = split(got)
        both = dot_nn(high, place) + dot_nn(low, place)
        ysend[q] = both[:, 128:]
        y_copy(q).start()
        mine[q] = both[:, :128]

    def z_copy(q, t):
        core = t % 2
        y = (t // 2) % 2
        i = 7 - t // 4
        z = (i % 2) * ((i + 1) // 2) + (1 - i % 2) * (8 - i // 2)
        zb = (b // 2 + z) % 8
        d = (((b // 16) + y) % 2 * 8 + zb) * 2 + (b + core) % 2
        rows = pltpu.make_async_remote_copy(
            src_ref=zsend.at[q, d],
            dst_ref=zrecv.at[q, b],
            send_sem=zs.at[q],
            recv_sem=zr.at[q],
            device_id=(d, c),
            device_id_type=MESH,
        )
        sums = pltpu.make_async_remote_copy(
            src_ref=csend.at[q],
            dst_ref=crecv.at[q, b],
            send_sem=cs.at[q],
            recv_sem=cr.at[q],
            device_id=(d, c),
            device_id_type=MESH,
        )
        return rows, sums

    def z_all(q, s_ref, r_ref, s_sem, r_sem):
        return pltpu.make_async_remote_copy(
            src_ref=s_ref.at[q, pl.ds(0, NB_PEERS)],
            dst_ref=r_ref.at[q, pl.ds(0, NB_PEERS)],
            send_sem=s_sem.at[q],
            recv_sem=r_sem.at[q],
            device_id=((b + 1) % 32, c),
            device_id_type=MESH,
        )

    def after_y(q):
        y_copy(q).wait_recv()
        block = mine[q] + yrecv[q]
        sums = jnp.sum(block, axis=0, keepdims=True)
        csend[q] = sums
        crecv[q, b] = sums
        high, low = split(block)
        packed = dot_nn(pack_rows[...], high) + dot_nn(pack_rows[...], low)
        zsend[q] = packed.reshape(32, 16, 128)
        zrecv[q, b] = zsend[q, b]

        def send(t, carry):
            rows, sums = z_copy(q, t)
            rows.start()
            sums.start()
            return carry

        lax.fori_loop(0, 28, send, 0)
        lax.fori_loop(29, 32, send, 0)

    weighted, row_sum, col_sum = [], [], []

    def after_z(q):
        z_all(q, zsend, zrecv, zs, zr).wait_recv()
        z_all(q, crecv, crecv, cs, cr).wait_recv()
        high, low = split(zrecv[q].reshape(512, 128))
        out = dot_nn(unpack_rows[...], high) + dot_nn(unpack_rows[...], low)
        merged[:, q * 128 : (q + 1) * 128] = out
        arriving = jnp.sum(crecv[q], axis=0)
        weighted.append(out * (jnp.log(out * 0.25) - jnp.log(arriving * (2.0**-14))))
        row_sum.append(out)
        col_sum.append(arriving)

    for step in range(NQ + 2):
        if step < NQ:
            after_x(step)
        if 0 <= step - 1 < NQ:
            after_y(step - 1)
        if 0 <= step - 2:
            after_z(step - 2)

    tsend[0:1] = jnp.sum(sum(weighted).T, axis=0, keepdims=True)
    tsend[1:2] = jnp.sum(sum(row_sum).T, axis=0, keepdims=True)
    tsend[2:3] = sum(col_sum)
    tsend[3:8] = jnp.zeros((5, 128), F32)
    trecv[0] = tsend[...]

    def t_copy(t):
        return pltpu.make_async_remote_copy(
            src_ref=tsend,
            dst_ref=trecv.at[t],
            send_sem=ts.at[t],
            recv_sem=tr.at[t],
            device_id=(b, (c + t) % 8),
            device_id_type=MESH,
        )

    for t in range(1, 8):
        t_copy(t).start()
    for t in range(1, 8):
        t_copy(t).wait_recv()
    everyone = jnp.sum(trecv[...], axis=0)
    out_total = everyone[1:2]
    total = jnp.sum(everyone[2:3], axis=1, keepdims=True)
    terms[...] = (
        everyone[0:1] / out_total
        + jnp.log(total * (2.0**-26))
        - jnp.log(out_total * (2.0**-14))
    )

    for q in range(NQ):
        for dx in range(1, 4):
            x_copy(q, dx).wait_send()
        y_copy(q).wait_send()
        z_all(q, zsend, zrecv, zs, zr).wait_send()
        z_all(q, crecv, crecv, cs, cr).wait_send()
    for t in range(1, 8):
        t_copy(t).wait_send()


def shards(counts, merge_map):
    ids = merge_map.reshape(32, 1, 256)
    dma = pltpu.SemaphoreType.DMA
    merged, terms = pl.pallas_call(
        kernel,
        out_shape=(
            jax.ShapeDtypeStruct((128, 512), F32),
            jax.ShapeDtypeStruct((1, 128), F32),
        ),
        in_specs=[
            pl.BlockSpec(memory_space=pl.ANY),
            pl.BlockSpec(memory_space=pltpu.VMEM),
        ],
        out_specs=(
            pl.BlockSpec(memory_space=pltpu.VMEM),
            pl.BlockSpec(memory_space=pltpu.VMEM),
        ),
        scratch_shapes=[
            pltpu.VMEM((256, 1024), F32),
            pltpu.VMEM((2, 256, 1024), BF16),
            pltpu.VMEM((32, 1, 256), I32),
            pltpu.VMEM((NQ, 4, 2, 4, 16, 1), F32),
            pltpu.VMEM((32, 16, 1), F32),
            pltpu.VMEM((128, 512), BF16),
            pltpu.VMEM((512, 256), BF16),
            pltpu.VMEM((NQ, 256, 128), F32),
            pltpu.VMEM((NQ, 4, 256, 128), F32),
            pltpu.VMEM((NQ, 4, 256, 128), F32),
            pltpu.VMEM((NQ, 256, 128), F32),
            pltpu.VMEM((NQ, 256, 128), F32),
            pltpu.VMEM((NQ, 32, 16, 128), F32),
            pltpu.VMEM((NQ, 32, 16, 128), F32),
            pltpu.VMEM((NQ, 1, 128), F32),
            pltpu.VMEM((NQ, 32, 1, 128), F32),
            pltpu.VMEM((8, 128), F32),
            pltpu.VMEM((8, 8, 128), F32),
            dma,
            dma((NQ, 4)),
            dma((NQ, 4)),
            dma((NQ,)),
            dma((NQ,)),
            dma((NQ,)),
            dma((NQ,)),
            dma((NQ,)),
            dma((NQ,)),
            dma((8,)),
            dma((8,)),
        ],
        compiler_params=pltpu.CompilerParams(
            collective_id=0, has_side_effects=True, vmem_limit_bytes=48 * 1024 * 1024
        ),
    )(counts, ids)
    return merged, terms.reshape(128)


def solution(mesh):
    return jax.shard_map(
        shards,
        mesh=mesh,
        in_specs=(P("blk", "col"), P()),
        out_specs=(P("blk", "col"), P("blk")),
        check_vma=False,
    )
```

time: 161 us -> 65.8 us (0.41)
  Pallas kernels: 0 us -> 61.8 us
  waiting for transfers between devices: 58.4 us -> 0 us
  blocking collectives: 57.4 us -> 0 us
  starting transfers between devices: 18.9 us -> 0 us
  matrix products: 10.7 us -> 0 us
  local copies, waits for them, and re-layouts: 8.58 us -> 3.19 us
  other arithmetic: 4.8 us -> 0 us
    pallas_call x0 -> x1, Pallas kernels: none -> 61.8 us  [shards(): pl.pallas_call(kernel, out_shape=(jax.ShapeDtypeStruct((128, 512), F32),...]
    all_to_all x3 -> x0, waiting for transfers between devices: 58.4 us -> none  [the longest x1 48.5 us: shards(): lax.all_to_all(buffer, 'blk', split_axis=0, concat_axis=0, tiled=True)]
    all_to_all x3 -> x0, blocking collectives: 57.4 us -> none  [the longest x1 33.4 us: sent_and_summed(): lax.all_to_all(blocks, axis, split_axis=0, concat_axis=0, tiled=True)]
    all_to_all x3 -> x0, starting transfers between devices: 18.9 us -> none  [the longest x1 11.1 us: shards(): lax.all_to_all(tags, 'blk', split_axis=0, concat_axis=0, tiled=True)]
    dot_general x2 -> x0, matrix products: 10.7 us -> none  [the longest x1 9.77 us: shards(): lax.dot_general(table, row_merged, (((0,), (1,)), ((), ())), precision=HI...]
    scatter x2 -> x0, local copies, waits for them, and re-layouts: 4.94 us -> none  [the longest x1 3.54 us: pack_rows(): jnp.zeros((groups * capacity, width), jnp.float32).at[target].set(matrix)]
    reduce_sum x6 -> x0, other arithmetic: 2.76 us -> none  [the longest x1 0.81 us: shards(): partial_terms = jnp.sum(share * jnp.log(ratio), axis=1)]
    unnamed x1 -> x6, local copies, waits for them, and re-layouts: 0.84 us -> 3.19 us
  transfers between devices with their start and end apart: 3 -> 0, of which waited for: 3 -> 0; matrix products, arithmetic and copies ran while one was open for 3% -> 0% of each run, Pallas kernels for 0% -> 0%
where the time goes in v1:
time: 65.8 us; the launch traced here: 65.6 us
  Pallas kernels  61.8 us (94%)
  local copies, waits for them, and re-layouts  3.19 us (5%)
    pallas_call x1, Pallas kernels, shards(): pl.pallas_call(kernel, out_shape=(jax.ShapeDtypeStruct((128, 512), F32),...  61.8 us
    unnamed x6, local copies, waits for them, and re-layouts  3.19 us

profile of v1, /device:TPU:1, one launch (start us, length us, event | category | flops | bytes accessed | tf_op | source)
XLA Modules:
  0.0 65.6 jit_solution(172253796140295130)
XLA Ops:
  0.6 0.0 copy-start
  0.6 1.2 %copy-done = f32[256,1024]{1,0:T(8,128)S(1)} copy-done((f32[256,1024]{1,0:T(8,128)S(1)}, f32[256,1024]{1,0:T(8,128)}, u32[]{:S(2)}) %copy-start) | copy-done | bytes 1048600
  1.9 0.0 copy-start.1
  1.9 0.8 %copy-done.1 = s32[8192,1]{0,1:T(1,128)S(1)} copy-done((s32[8192,1]{0,1:T(1,128)S(1)}, s32[8192,1]{0,1:T(1,128)}, u32[]{:S(2)}) %copy-start.1) | copy-done | bytes 32792
  2.6 61.8 %shard_map.41 = (f32[128,512]{1,0:T(8,128)S(1)}, f32[1,128]{1,0:T(1,128)S(1)}) custom-call(f32[256,1024]{1,0:T(8,128)S(1)} %copy-done, s32[32,1,256]{2,1,0:T(1,128)S(1)} %bitcast.2), custom_call_target="tpu_custom_call" | custom-call | tf_op jit(solution)/shard_map/pallas_call | solution.py:318
  64.4 0.7 %copy.6 = f32[128,512]{1,0:T(8,128)} copy(f32[128,512]{1,0:T(8,128)S(1)} %get-tuple-element.8) | data formatting | bytes 524288
  65.1 0.5 copy.7
Async XLA Ops:
  0.6 1.2 %copy-start = (f32[256,1024]{1,0:T(8,128)S(1)}, f32[256,1024]{1,0:T(8,128)}, u32[]{:S(2)}) copy-start(f32[256,1024]{1,0:T(8,128)} %counts_hbm.1) | copy-start | bytes 3145732
  1.9 0.8 %copy-start.1 = (s32[8192,1]{0,1:T(1,128)S(1)}, s32[8192,1]{0,1:T(1,128)}, u32[]{:S(2)}) copy-start(s32[8192,1]{0,1:T(1,128)} %param.3) | copy-start | bytes 98308

commit v2 on v1

v2 whole, which is shorter than its diff:
```python
import jax
import jax.numpy as jnp
from jax import lax
from jax.experimental import pallas as pl
from jax.experimental.pallas import tpu as pltpu
from jax.sharding import PartitionSpec as P

MESH = pl.DeviceIdType.MESH
F32 = jnp.float32
BF16 = jnp.bfloat16
I32 = jnp.int32
NQ = 4
NP = 4
Z_STEPS = (4, 3, 5, 0, 2, 6, 1, 7)
DIRECT = ()
RELAYED = (0, 1, 2, 3)
ND, NR = len(DIRECT), len(RELAYED)
ORDER = (
    "tokens",
    "p2",
    "x0",
    "p3",
    "tags",
    "a0",
    "x1",
    "b0",
    "c0",
    "d0",
    "x2",
    "a1",
    "b1",
    "c1",
    "d1",
    "z0",
    "x3",
    "a2",
    "b2",
    "c2",
    "d2",
    "z1",
    "a3",
    "b3",
    "c3",
    "d3",
    "z2",
    "z3",
)


def split(v):
    high = v.astype(BF16)
    return high, (v - high.astype(F32)).astype(BF16)


def dot_nn(a, b):
    return lax.dot_general(a, b, (((1,), (0,)), ((), ())), preferred_element_type=F32)


def dot_nt(a, b):
    return lax.dot_general(a, b, (((1,), (1,)), ((), ())), preferred_element_type=F32)


def iota(shape, dim):
    return lax.broadcasted_iota(I32, shape, dim)


def one_hot(mask):
    return jnp.where(mask, 1.0, 0.0).astype(BF16)


def slot_keys(rows):
    owners = [lax.shift_right_logical(r, 7) for r in rows]
    hits = [o == iota((32, 256), 0) for o in owners]
    table = jnp.concatenate([jnp.where(h, 1.0, 0.0) for h in hits], axis=0)
    before = one_hot(iota((256, 256), 0) < iota((256, 256), 1))
    counted = dot_nn(table.astype(BF16), before) * table
    ranks = [
        jnp.sum(counted[i * 32 : (i + 1) * 32], axis=0, keepdims=True).astype(I32)
        for i in range(len(rows))
    ]
    return [o * 16 + r for o, r in zip(owners, ranks)]


def kernel(
    counts_hbm,
    ids_hbm,
    merged,
    terms,
    counts,
    ids,
    parts,
    keys,
    nearby,
    coltag,
    rowtag,
    unpack_rows,
    pack_rows,
    dsend,
    drecv,
    xsend,
    xrecv,
    asend,
    arecv,
    bsend,
    brecv,
    zsend,
    zrecv,
    csend,
    crecv,
    tsend,
    trecv,
    in_sem,
    ids_sem,
    ds,
    dr,
    xs,
    xr,
    ys,
    yr,
    zs,
    zr,
    cs,
    cr,
    ts,
    tr,
    token,
):
    b = lax.axis_index("blk")
    c = lax.axis_index("col")
    x, yh = lax.rem(c, 4), lax.div(c, 4)
    core, zz, yl = lax.rem(b, 2), lax.rem(lax.div(b, 2), 8), lax.div(b, 16)

    ids_load = pltpu.make_async_copy(ids_hbm, ids, ids_sem)
    ids_load.start()
    load = pltpu.make_async_copy(counts_hbm, counts, in_sem)
    load.start()

    barrier = pltpu.get_barrier_semaphore()

    def z_peer(step, k):
        return (yl * 8 + lax.rem(zz + step, 8)) * 2 + lax.rem(core + k, 2)

    def y_peer(p, r):
        return lax.rem(yl + r, 2) * 16 + zz * 2 + core, lax.rem(c + 4 * p, 8)

    def greet(peer):
        pl.semaphore_signal(barrier, inc=1, device_id=peer, device_id_type=MESH)

    for dx in range(1, 4):
        greet((b, yh * 4 + lax.rem(x + dx, 4)))
    for p, r in ((1, 0), (0, 1), (1, 1)):
        greet(y_peer(p, r))
    for step, k in ((1, 0), (7, 0), (0, 1)):
        greet((z_peer(step, k), c))

    ids_load.wait()
    positions = []
    for g, key in enumerate(slot_keys([ids[c * 4 + g] for g in range(4)])):
        owner = lax.shift_right_logical(key, 4)
        to = lax.shift_right_logical(owner, 2)
        dx = (to - x) & 3
        tile = jnp.where(dx == 2, 0, jnp.where(dx == 1, 1, jnp.where(dx == 3, 2, 3)))
        half = (lax.shift_right_logical(to, 2) - yh) & 1
        positions.append((owner & 3) * 512 + tile * 128 + half * 64 + g * 16 + (key & 15))
    position = jnp.concatenate(positions, axis=1)

    load.wait()
    high, low = split(counts[...])
    parts[0] = high
    parts[1] = low

    def x_copy(q, dx):
        return pltpu.make_async_remote_copy(
            src_ref=xsend.at[q, dx],
            dst_ref=xrecv.at[q, dx],
            send_sem=xs.at[q, dx],
            recv_sem=xr.at[q, dx],
            device_id=(b, yh * 4 + lax.rem(x + dx, 4)),
            device_id_type=MESH,
        )

    def d_copy(q, p, dx):
        return pltpu.make_async_remote_copy(
            src_ref=dsend.at[q, p, dx],
            dst_ref=drecv.at[q, p, dx],
            send_sem=ds.at[q, p, dx],
            recv_sem=dr.at[q, p, dx],
            device_id=(b, lax.rem(yh + p, 2) * 4 + lax.rem(x + dx, 4)),
            device_id_type=MESH,
        )

    first_half = iota((128, 128), 1) < 64

    def pack(q):
        for first, tiles in ((0, (2, 1)), (256, (3, 0))):
            pick = one_hot(position - q * 512 == iota((256, 1024), 0) + first)
            packed = dot_nt(parts[0], pick) + dot_nt(parts[1], pick)
            for i, dx in enumerate(tiles):
                value = packed[:, i * 128 : (i + 1) * 128]
                if q in DIRECT:
                    at = DIRECT.index(q)
                    top, bottom = value[:128], value[128:]
                    for p in (1, 0):
                        if p:
                            both = jnp.where(first_half, pltpu.roll(top, 64, 1), bottom)
                        else:
                            both = jnp.where(first_half, top, pltpu.roll(bottom, 64, 1))
                        if p == 0 and dx == 0:
                            drecv[at, 0, 0] = both
                        else:
                            dsend[at, p, dx] = both
                else:
                    at = RELAYED.index(q)
                    if dx == 0:
                        xrecv[at, 0] = value
                    else:
                        xsend[at, dx] = value
            if q > 0:
                send_columns(q, tiles)

    def send_columns(q, tiles):
        for dx in tiles:
            if q in DIRECT:
                for p in (1, 0):
                    if p or dx:
                        d_copy(DIRECT.index(q), p, dx).start()
            elif dx:
                x_copy(RELAYED.index(q), dx).start()


    sixteen = iota((16, 1), 0)

    def pass_token(i):
        for way, step in enumerate((1, 7)):
            pl.semaphore_signal(
                token.at[i, way], inc=1, device_id=(z_peer(step, 0), c), device_id_type=MESH
            )

    def take_token(i):
        for way in range(2):
            pl.semaphore_wait(token.at[i, way], 1)


    def all_keys():
        for i in range(4):
            for g, key in enumerate(slot_keys([ids[i * 8 + g] for g in range(8)])):
                keys[i * 8 + g] = key

    def column_tags():
        near = [c * 4 + q for q in DIRECT]
        far = [(lax.rem(yh + p, 2) * 4 + x) * 4 + q for q in RELAYED for p in range(2)]
        for p in range(2):
            owners = near + far if p == 0 else near
            if not owners:
                continue
            wanted = jnp.concatenate([o * 16 + sixteen for o in owners], axis=0)
            for dx in range(4):
                for g in range(4):
                    src = lax.rem(yh + p, 2) * 16 + lax.rem(x + 4 - dx, 4) * 4 + g
                    value = ((ids[src] & 127) + 1).astype(F32)
                    tag = jnp.sum(
                        jnp.where(keys[src] == wanted, value, 0.0), axis=1, keepdims=True
                    )
                    other = jnp.where(tag > 0.0, tag + 128.0, 0.0)
                    for i in range(ND):
                        nearby[i, p, dx, 0, g] = tag[i * 16 : i * 16 + 16]
                        nearby[i, p, dx, 1, g] = other[i * 16 : i * 16 + 16]
                    if p == 0:
                        for i in range(NR):
                            at = ND * 16 + i * 32
                            coltag[i, dx, 0, g] = tag[at : at + 16]
                            coltag[i, dx, 1, g] = other[at + 16 : at + 32]

    def row_places():
        key = keys[b]
        owner = lax.shift_right_logical(key, 4)
        k = (owner - core) & 1
        dz = (lax.shift_right_logical(owner, 1) - zz) & 7
        r = (lax.shift_right_logical(owner, 4) - yl) & 1
        at = sum(jnp.where(dz == step, i, 0) for i, step in enumerate(Z_STEPS))
        place = (at >> 1) * 128 + r * 64 + (at & 1) * 32 + k * 16 + (key & 15)
        pack_rows[...] = one_hot(place == iota((512, 256), 0))

    def row_tags():
        for i, step in enumerate(Z_STEPS):
            for k in range(2):
                for r in range(2):
                    z = lax.rem(zz + 8 - step, 8)
                    src = (lax.rem(yl + r, 2) * 8 + z) * 2 + lax.rem(core + k, 2)
                    value = ((ids[src] & 127) + 1).astype(F32)
                    hit = keys[src] == b * 16 + sixteen
                    rowtag[(i * 2 + k) * 2 + r] = jnp.sum(
                        jnp.where(hit, value, 0.0), axis=1, keepdims=True
                    )
        flat = rowtag[...].reshape(512, 1).astype(I32)
        unpack_rows[...] = jnp.where(flat == iota((512, 128), 1) + 1, 1.0, 0.0).T.astype(BF16)

    pack(0)
    pl.semaphore_wait(barrier, 9)
    send_columns(0, (2, 1, 3, 0))
    pass_token(0)
    pack(1)
    all_keys()
    column_tags()
    row_places()

    def y_peers(q):
        return ((0, 1),) if q in DIRECT else ((1, 0), (1, 1), (0, 1))

    def y_refs(q, part):
        if part == 0:
            return asend.at[q], arecv.at[q]
        return bsend.at[q, part - 1], brecv.at[q, part - 1]

    def y_copy(q, part, p, r):
        src, dst = y_refs(q, part)
        return pltpu.make_async_remote_copy(
            src_ref=src.at[p, r],
            dst_ref=dst.at[p, r],
            send_sem=ys.at[q, part, p, r],
            recv_sem=yr.at[q, part, p, r],
            device_id=y_peer(p, r),
            device_id_type=MESH,
        )

    def after_x(q):
        i = RELAYED.index(q)
        tag = coltag[i].reshape(512, 1).astype(I32)
        place = one_hot(tag == iota((512, 256), 1) + 1)
        for dx in range(1, 4):
            x_copy(i, dx).wait_recv()
        got = jnp.concatenate([xrecv[i, dx] for dx in range(4)], axis=1)
        high, low = split(got)
        send_y(q, dot_nn(high, place) + dot_nn(low, place), 2)

    def after_d(q):
        i = DIRECT.index(q)
        tag = nearby[i].reshape(1024, 1).astype(I32)
        place = one_hot(tag == iota((1024, 256), 1) + 1)
        for p in range(2):
            for dx in range(4):
                if p or dx:
                    d_copy(i, p, dx).wait_recv()
        got = jnp.concatenate([drecv[i, p, dx] for p in range(2) for dx in range(4)], axis=1)
        high, low = split(got)
        both = dot_nn(high, place) + dot_nn(low, place)
        send_y(q, jnp.concatenate([both[:, :128], both[:, 128:]], axis=0), 1)

    def send_y(q, block, halves):
        sums = jnp.sum(block, axis=0, keepdims=True)
        high, low = split(block)
        for part in range(NP):
            pick = pack_rows[part * 128 : (part + 1) * 128]
            packed = dot_nn(pick, high) + dot_nn(pick, low)
            out = y_refs(q, part)[0]
            for p in range(halves):
                for r in range(2):
                    at = r * 64
                    out[p, r, 0:64] = packed[at : at + 64, p * 128 : (p + 1) * 128]
                    if part == 0:
                        out[p, r, 64:72] = jnp.broadcast_to(
                            sums[:, p * 128 : (p + 1) * 128], (8, 128)
                        )
            for p, r in y_peers(q):
                y_copy(q, part, p, r).start()

    def to_z(step, k, src, dst, send, recv):
        return pltpu.make_async_remote_copy(
            src_ref=src,
            dst_ref=dst,
            send_sem=send,
            recv_sem=recv,
            device_id=(z_peer(step, k), c),
            device_id_type=MESH,
        )

    def all_rows(q, part):
        few = pl.ds(0, 4 - (1 if part == 1 else 0))
        return to_z(
            1, 0, zsend.at[q, part, few], zrecv.at[q, part, few], zs.at[q, part], zr.at[q, part]
        )

    def all_sums(q):
        few = pl.ds(0, 15)
        return to_z(1, 0, crecv.at[q, few], crecv.at[q, few], cs.at[q], cr.at[q])

    def after_y(q, part):
        for p, r in y_peers(q):
            y_copy(q, part, p, r).wait_recv()
        own, got = y_refs(q, part)
        if part == 0:
            csend[q] = own[0, 0, 64:65] + sum(got[p, r, 64:65] for p, r in y_peers(q))
            crecv[q, 15] = csend[q]
            for i, step in enumerate(Z_STEPS):
                for k in range(2):
                    if step or k:
                        at = i * 2 + k - (1 if i * 2 + k > 6 else 0)
                        to_z(step, k, csend.at[q], crecv.at[q, at], cs.at[q], cr.at[q]).start()
        mine, theirs = own[0, 0, 0:64], got[0, 1, 0:64]
        if q not in DIRECT:
            mine, theirs = mine + got[1, 0, 0:64], theirs + got[1, 1, 0:64]
        zsend[q, part, :, 0] = mine.reshape(4, 16, 128)
        zsend[q, part, :, 1] = theirs.reshape(4, 16, 128)
        for i in range(2):
            step = Z_STEPS[part * 2 + i]
            for k in range(2):
                at = i * 2 + k
                if step or k:
                    to_z(
                        step,
                        k,
                        zsend.at[q, part, at],
                        zrecv.at[q, part, at],
                        zs.at[q, part],
                        zr.at[q, part],
                    ).start()
                else:
                    zrecv[q, part, at] = zsend[q, part, at]

    weighted, row_sum, col_sum = [], [], []

    def after_z(q):
        all_sums(q).wait_recv()
        arriving = jnp.sum(crecv[q], axis=0)
        scale = jnp.log(arriving * (2.0**-14))
        for part in range(NP):
            all_rows(q, part).wait_recv()
        high, low = split(zrecv[q].reshape(512, 128))
        out = dot_nn(unpack_rows[...], high) + dot_nn(unpack_rows[...], low)
        merged[:, q * 128 : (q + 1) * 128] = out
        weighted.append(out * (jnp.log(out * 0.25) - scale))
        row_sum.append(out)
        col_sum.append(arriving)

    def go(step):
        kind, q = step[0], int(step[1])
        if kind == "p":
            pack(q)
        elif kind == "x":
            (after_d if q in DIRECT else after_x)(q)
        elif kind == "z":
            after_z(q)
        else:
            after_y(q, "abcd".index(kind))

    for step in ORDER:
        if step == "tags":
            row_tags()
        elif step == "tokens":
            for i in range(4):
                take_token(i)
                if i < 3:
                    pass_token(i + 1)
        else:
            go(step)

    tsend[0:1] = jnp.sum(sum(weighted).T, axis=0, keepdims=True)
    tsend[1:2] = jnp.sum(sum(row_sum).T, axis=0, keepdims=True)
    tsend[2:3] = sum(col_sum)
    tsend[3:8] = jnp.zeros((5, 128), F32)
    trecv[0] = tsend[...]

    def t_copy(t):
        return pltpu.make_async_remote_copy(
            src_ref=tsend,
            dst_ref=trecv.at[t],
            send_sem=ts,
            recv_sem=tr.at[t],
            device_id=(b, lax.rem(c + t, 8)),
            device_id_type=MESH,
        )

    all_told = pltpu.make_async_remote_copy(
        src_ref=trecv.at[pl.ds(0, 7)],
        dst_ref=trecv.at[pl.ds(0, 7)],
        send_sem=ts,
        recv_sem=tr.at[0],
        device_id=(b, lax.rem(c + 1, 8)),
        device_id_type=MESH,
    )
    for t in range(1, 8):
        t_copy(t).start()
    for q in range(NQ):
        for dx in range(4):
            if q in RELAYED:
                if dx:
                    x_copy(RELAYED.index(q), dx).wait_send()
            else:
                for p in range(2):
                    if p or dx:
                        d_copy(DIRECT.index(q), p, dx).wait_send()
        for part in range(NP):
            for p, r in y_peers(q):
                y_copy(q, part, p, r).wait_send()
            all_rows(q, part).wait_send()
        all_sums(q).wait_send()
    for t in range(1, 8):
        t_copy(t).wait_recv()
    all_told.wait_send()
    everyone = jnp.sum(trecv[...], axis=0)
    out_total = everyone[1:2]
    total = jnp.sum(everyone[2:3], axis=1, keepdims=True)
    terms[...] = (
        everyone[0:1] / out_total
        + jnp.log(total * (2.0**-26))
        - jnp.log(out_total * (2.0**-14))
    )


def shards(counts, merge_map):
    ids = merge_map.reshape(32, 1, 256)
    dma = pltpu.SemaphoreType.DMA
    merged, terms = pl.pallas_call(
        kernel,
        out_shape=(
            jax.ShapeDtypeStruct((128, 512), F32),
            jax.ShapeDtypeStruct((1, 128), F32),
        ),
        in_specs=[
            pl.BlockSpec(memory_space=pltpu.HBM),
            pl.BlockSpec(memory_space=pltpu.HBM),
        ],
        out_specs=(
            pl.BlockSpec(memory_space=pltpu.VMEM),
            pl.BlockSpec(memory_space=pltpu.VMEM),
        ),
        scratch_shapes=[
            pltpu.VMEM((256, 1024), F32),
            pltpu.VMEM((32, 1, 256), I32),
            pltpu.VMEM((2, 256, 1024), BF16),
            pltpu.VMEM((32, 1, 256), I32),
            pltpu.VMEM((max(ND, 1), 2, 4, 2, 4, 16, 1), F32),
            pltpu.VMEM((max(NR, 1), 4, 2, 4, 16, 1), F32),
            pltpu.VMEM((32, 16, 1), F32),
            pltpu.VMEM((128, 512), BF16),
            pltpu.VMEM((512, 256), BF16),
            pltpu.VMEM((max(ND, 1), 2, 4, 128, 128), F32),
            pltpu.VMEM((max(ND, 1), 2, 4, 128, 128), F32),
            pltpu.VMEM((max(NR, 1), 4, 256, 128), F32),
            pltpu.VMEM((max(NR, 1), 4, 256, 128), F32),
            pltpu.VMEM((NQ, 2, 2, 72, 128), F32),
            pltpu.VMEM((NQ, 2, 2, 72, 128), F32),
            pltpu.VMEM((NQ, NP - 1, 2, 2, 64, 128), F32),
            pltpu.VMEM((NQ, NP - 1, 2, 2, 64, 128), F32),
            pltpu.VMEM((NQ, NP, 4, 2, 16, 128), F32),
            pltpu.VMEM((NQ, NP, 4, 2, 16, 128), F32),
            pltpu.VMEM((NQ, 1, 128), F32),
            pltpu.VMEM((NQ, 16, 1, 128), F32),
            pltpu.VMEM((8, 128), F32),
            pltpu.VMEM((8, 8, 128), F32),
            dma,
            dma,
            dma((max(ND, 1), 2, 4)),
            dma((max(ND, 1), 2, 4)),
            dma((max(NR, 1), 4)),
            dma((max(NR, 1), 4)),
            dma((NQ, NP, 2, 2)),
            dma((NQ, NP, 2, 2)),
            dma((NQ, NP)),
            dma((NQ, NP)),
            dma((NQ,)),
            dma((NQ,)),
            dma,
            dma((8,)),
            pltpu.SemaphoreType.REGULAR((4, 2)),
        ],
        compiler_params=pltpu.CompilerParams(
            collective_id=0, has_side_effects=True, vmem_limit_bytes=56_000_000
        ),
    )(counts, ids)
    return merged, terms.reshape(128)


def solution(mesh):
    return jax.shard_map(
        shards,
        mesh=mesh,
        in_specs=(P("blk", "col"), P()),
        out_specs=(P("blk", "col"), P("blk")),
        check_vma=False,
    )
```

time: 65.8 us -> 58.6 us (0.89)
  Pallas kernels: 61.8 us -> 55.8 us
  local copies, waits for them, and re-layouts: 3.19 us -> 1.97 us
    pallas_call x1, Pallas kernels: 61.8 us -> 55.8 us  [shards(): pl.pallas_call(kernel, out_shape=(jax.ShapeDtypeStruct((128, 512), F32),...]
    unnamed x6 -> x4, local copies, waits for them, and re-layouts: 3.19 us -> 1.97 us
where the time goes in v2:
time: 58.6 us; the launch traced here: 58.4 us
  Pallas kernels  55.8 us (95%)
  local copies, waits for them, and re-layouts  1.97 us (3%)
  between operations  0.65 us (1%)
    pallas_call x1, Pallas kernels, shards(): pl.pallas_call(kernel, out_shape=(jax.ShapeDtypeStruct((128, 512), F32),...  55.8 us
    unnamed x4, local copies, waits for them, and re-layouts  1.97 us

profile of v2, /device:TPU:1, one launch (start us, length us, event | category | flops | bytes accessed | tf_op | source)
XLA Modules:
  0.0 58.4 jit_solution(1438658024296307927)
XLA Ops:
  0.6 0.0 copy-start
  0.6 0.7 %copy-done = s32[8192,1]{0,1:T(1,128)S(1)} copy-done((s32[8192,1]{0,1:T(1,128)S(1)}, s32[8192,1]{0,1:T(1,128)}, u32[]{:S(2)}) %copy-start) | copy-done | bytes 32792
  1.4 55.8 %shard_map.41 = (f32[128,512]{1,0:T(8,128)S(1)}, f32[1,128]{1,0:T(1,128)S(1)}) custom-call(f32[256,1024]{1,0:T(8,128)} %counts_hbm.1, s32[32,1,256]{2,1,0:T(1,128)S(1)} %bitcast.2), custom_call_target="tpu_custom_call" | custom-call | tf_op jit(solution)/shard_map/pallas_call | solution.py:513
  57.2 0.7 %copy.6 = f32[128,512]{1,0:T(8,128)} copy(f32[128,512]{1,0:T(8,128)S(1)} %get-tuple-element.8) | data formatting | bytes 524288
  57.9 0.5 copy.7
Async XLA Ops:
  0.6 0.8 %copy-start = (s32[8192,1]{0,1:T(1,128)S(1)}, s32[8192,1]{0,1:T(1,128)}, u32[]{:S(2)}) copy-start(s32[8192,1]{0,1:T(1,128)} %param.3) | copy-start | bytes 98308

commit v3 on v2

v3 whole, which is shorter than its diff:
```python
import jax
import jax.numpy as jnp
from jax import lax
from jax.experimental import pallas as pl
from jax.experimental.pallas import tpu as pltpu
from jax.sharding import PartitionSpec as P

MESH = pl.DeviceIdType.MESH
F32 = jnp.float32
BF16 = jnp.bfloat16
I32 = jnp.int32
NQ = 4
NP = 4
Z_STEPS = (4, 3, 5, 0, 2, 6, 1, 7)
ORDER = (
    "tokens",
    "p2",
    "x0",
    "p3",
    "tags",
    "a0",
    "x1",
    "b0",
    "c0",
    "d0",
    "x2",
    "a1",
    "b1",
    "c1",
    "d1",
    "z0",
    "x3",
    "a2",
    "b2",
    "c2",
    "d2",
    "z1",
    "a3",
    "b3",
    "c3",
    "d3",
    "z2",
    "z3",
)


def split(v):
    high = v.astype(BF16)
    return high, (v - high.astype(F32)).astype(BF16)


def dot_nn(a, b):
    return lax.dot_general(a, b, (((1,), (0,)), ((), ())), preferred_element_type=F32)


def dot_nt(a, b):
    return lax.dot_general(a, b, (((1,), (1,)), ((), ())), preferred_element_type=F32)


def iota(shape, dim):
    return lax.broadcasted_iota(I32, shape, dim)


def one_hot(mask):
    return jnp.where(mask, 1.0, 0.0).astype(BF16)


def slot_keys(rows):
    owners = [lax.shift_right_logical(r, 7) for r in rows]
    hits = [o == iota((32, 256), 0) for o in owners]
    table = jnp.concatenate([jnp.where(h, 1.0, 0.0) for h in hits], axis=0)
    before = one_hot(iota((256, 256), 0) < iota((256, 256), 1))
    counted = dot_nn(table.astype(BF16), before) * table
    ranks = [
        jnp.sum(counted[i * 32 : (i + 1) * 32], axis=0, keepdims=True).astype(I32)
        for i in range(len(rows))
    ]
    return [o * 16 + r for o, r in zip(owners, ranks)]


def kernel(
    counts_hbm,
    ids_hbm,
    merged,
    terms,
    counts,
    ids,
    parts,
    keys,
    coltag,
    rowtag,
    unpack_rows,
    pack_rows,
    xsend,
    xrecv,
    asend,
    arecv,
    bsend,
    brecv,
    zsend,
    zrecv,
    csend,
    crecv,
    tsend,
    trecv,
    in_sem,
    ids_sem,
    xs,
    xr,
    ys,
    yr,
    zs,
    zr,
    cs,
    cr,
    ts,
    tr,
    token,
):
    b = lax.axis_index("blk")
    c = lax.axis_index("col")
    x, yh = lax.rem(c, 4), lax.div(c, 4)
    core, zz, yl = lax.rem(b, 2), lax.rem(lax.div(b, 2), 8), lax.div(b, 16)

    ids_load = pltpu.make_async_copy(ids_hbm, ids, ids_sem)
    ids_load.start()
    load = pltpu.make_async_copy(counts_hbm, counts, in_sem)
    load.start()

    barrier = pltpu.get_barrier_semaphore()

    def z_peer(step, k):
        return (yl * 8 + lax.rem(zz + step, 8)) * 2 + lax.rem(core + k, 2)

    def y_peer(p, r):
        return lax.rem(yl + r, 2) * 16 + zz * 2 + core, lax.rem(c + 4 * p, 8)

    def greet(peer):
        pl.semaphore_signal(barrier, inc=1, device_id=peer, device_id_type=MESH)

    for dx in range(1, 4):
        greet((b, yh * 4 + lax.rem(x + dx, 4)))
    for p, r in ((1, 0), (0, 1), (1, 1)):
        greet(y_peer(p, r))
    for step, k in ((1, 0), (7, 0), (0, 1)):
        greet((z_peer(step, k), c))

    ids_load.wait()
    positions = []
    for g, key in enumerate(slot_keys([ids[c * 4 + g] for g in range(4)])):
        owner = lax.shift_right_logical(key, 4)
        to = lax.shift_right_logical(owner, 2)
        dx = (to - x) & 3
        tile = jnp.where(dx == 2, 0, jnp.where(dx == 1, 1, jnp.where(dx == 3, 2, 3)))
        half = (lax.shift_right_logical(to, 2) - yh) & 1
        positions.append((owner & 3) * 512 + tile * 128 + half * 64 + g * 16 + (key & 15))
    position = jnp.concatenate(positions, axis=1)

    load.wait()
    high, low = split(counts[...])
    parts[0] = high
    parts[1] = low

    def x_copy(q, dx):
        return pltpu.make_async_remote_copy(
            src_ref=xsend.at[q, dx],
            dst_ref=xrecv.at[q, dx],
            send_sem=xs,
            recv_sem=xr.at[q],
            device_id=(b, yh * 4 + lax.rem(x + dx, 4)),
            device_id_type=MESH,
        )

    def all_columns(refs, recv):
        return pltpu.make_async_remote_copy(
            src_ref=refs,
            dst_ref=refs,
            send_sem=xs,
            recv_sem=recv,
            device_id=(b, yh * 4 + lax.rem(x + 1, 4)),
            device_id_type=MESH,
        )

    def pack(q):
        for first, tiles in ((0, (2, 1)), (256, (3, 0))):
            pick = one_hot(position - q * 512 == iota((256, 1024), 0) + first)
            packed = dot_nt(parts[0], pick) + dot_nt(parts[1], pick)
            for i, dx in enumerate(tiles):
                value = packed[:, i * 128 : (i + 1) * 128]
                if dx == 0:
                    xrecv[q, 0] = value
                else:
                    xsend[q, dx] = value
                    if q > 0:
                        x_copy(q, dx).start()

    sixteen = iota((16, 1), 0)

    def pass_token():
        for way, step in enumerate((1, 7)):
            pl.semaphore_signal(
                token.at[way], inc=1, device_id=(z_peer(step, 0), c), device_id_type=MESH
            )

    def take_token():
        for way in range(2):
            pl.semaphore_wait(token.at[way], 1)


    def all_keys():
        for i in range(4):
            for g, key in enumerate(slot_keys([ids[i * 8 + g] for g in range(8)])):
                keys[i * 8 + g] = key

    def column_tags():
        owners = [(lax.rem(yh + p, 2) * 4 + x) * 4 + q for q in range(NQ) for p in range(2)]
        wanted = jnp.concatenate([o * 16 + sixteen for o in owners], axis=0)
        for dx in range(4):
            for g in range(4):
                src = yh * 16 + lax.rem(x + 4 - dx, 4) * 4 + g
                value = ((ids[src] & 127) + 1).astype(F32)
                tag = jnp.sum(jnp.where(keys[src] == wanted, value, 0.0), axis=1, keepdims=True)
                other = jnp.where(tag > 0.0, tag + 128.0, 0.0)
                for q in range(NQ):
                    coltag[q, dx, 0, g] = tag[q * 32 : q * 32 + 16]
                    coltag[q, dx, 1, g] = other[q * 32 + 16 : q * 32 + 32]

    def row_places():
        key = keys[b]
        owner = lax.shift_right_logical(key, 4)
        k = (owner - core) & 1
        dz = (lax.shift_right_logical(owner, 1) - zz) & 7
        r = (lax.shift_right_logical(owner, 4) - yl) & 1
        at = sum(jnp.where(dz == step, i, 0) for i, step in enumerate(Z_STEPS))
        place = (at >> 1) * 128 + r * 64 + (at & 1) * 32 + k * 16 + (key & 15)
        pack_rows[...] = one_hot(place == iota((512, 256), 0))

    def row_tags():
        for i, step in enumerate(Z_STEPS):
            for k in range(2):
                for r in range(2):
                    z = lax.rem(zz + 8 - step, 8)
                    src = (lax.rem(yl + r, 2) * 8 + z) * 2 + lax.rem(core + k, 2)
                    value = ((ids[src] & 127) + 1).astype(F32)
                    hit = keys[src] == b * 16 + sixteen
                    rowtag[(i * 2 + k) * 2 + r] = jnp.sum(
                        jnp.where(hit, value, 0.0), axis=1, keepdims=True
                    )
        flat = rowtag[...].reshape(512, 1).astype(I32)
        unpack_rows[...] = jnp.where(flat == iota((512, 128), 1) + 1, 1.0, 0.0).T.astype(BF16)

    pack(0)
    pl.semaphore_wait(barrier, 9)
    for dx in (2, 1, 3):
        x_copy(0, dx).start()
    pass_token()
    pack(1)
    all_keys()
    column_tags()
    row_places()

    Y_PEERS = ((1, 0), (1, 1), (0, 1))

    def y_refs(q, part):
        if part == 0:
            return asend.at[q], arecv.at[q]
        return bsend.at[q, part - 1], brecv.at[q, part - 1]

    def y_copy(q, part, p, r, few=False):
        src, dst = y_refs(q, part)
        at = pl.ds(0, 3) if few else p * 2 + r
        return pltpu.make_async_remote_copy(
            src_ref=src.at[at],
            dst_ref=dst.at[at],
            send_sem=ys.at[min(part, 1)],
            recv_sem=yr.at[q, part],
            device_id=y_peer(p, r),
            device_id_type=MESH,
        )

    def after_x(q):
        tag = coltag[q].reshape(512, 1).astype(I32)
        place = one_hot(tag == iota((512, 256), 1) + 1)
        all_columns(xrecv.at[q, pl.ds(0, 3)], xr.at[q]).wait_recv()
        got = jnp.concatenate([xrecv[q, dx] for dx in range(4)], axis=1)
        high, low = split(got)
        block = dot_nn(high, place) + dot_nn(low, place)
        sums = jnp.sum(block, axis=0, keepdims=True)
        high, low = split(block)
        for part in range(NP):
            pick = pack_rows[part * 128 : (part + 1) * 128]
            packed = dot_nn(pick, high) + dot_nn(pick, low)
            out = y_refs(q, part)[0]
            for p in range(2):
                for r in range(2):
                    at = r * 64
                    out[p * 2 + r, 0:64] = packed[at : at + 64, p * 128 : (p + 1) * 128]
                    if part == 0:
                        out[p * 2 + r, 64:72] = jnp.broadcast_to(
                            sums[:, p * 128 : (p + 1) * 128], (8, 128)
                        )
            for p, r in Y_PEERS:
                y_copy(q, part, p, r).start()

    def all_sends(refs, send):
        return pltpu.make_async_remote_copy(
            src_ref=refs,
            dst_ref=refs,
            send_sem=send,
            recv_sem=yr.at[0, 0],
            device_id=y_peer(0, 1),
            device_id_type=MESH,
        )

    def to_z(step, k, src, dst, send, recv):
        return pltpu.make_async_remote_copy(
            src_ref=src,
            dst_ref=dst,
            send_sem=send,
            recv_sem=recv,
            device_id=(z_peer(step, k), c),
            device_id_type=MESH,
        )

    def all_rows(refs, recv):
        return to_z(1, 0, refs, refs, zs, recv)

    def all_sums(refs, recv):
        return to_z(1, 0, refs, refs, cs, recv)

    def after_y(q, part):
        y_copy(q, part, 1, 0, few=True).wait_recv()
        own, got = y_refs(q, part)
        to = (q * NP + part) * 4
        if part == 0:
            csend[q] = own[0, 64:65] + got[1, 64:65] + got[2, 64:65] + got[3, 64:65]
            crecv[q * 16 + 15] = csend[q]
            for i, step in enumerate(Z_STEPS):
                for k in range(2):
                    if step or k:
                        at = q * 16 + i * 2 + k - (1 if i * 2 + k > 6 else 0)
                        to_z(step, k, csend.at[q], crecv.at[at], cs, cr.at[q]).start()
        mine = own[0, 0:64] + got[2, 0:64]
        theirs = got[1, 0:64] + got[3, 0:64]
        zsend[to : to + 4, 0] = mine.reshape(4, 16, 128)
        zsend[to : to + 4, 1] = theirs.reshape(4, 16, 128)
        for i in range(2):
            step = Z_STEPS[part * 2 + i]
            for k in range(2):
                at = to + i * 2 + k
                if step or k:
                    to_z(step, k, zsend.at[at], zrecv.at[at], zs, zr.at[q]).start()
                else:
                    zrecv[at] = zsend[at]

    weighted, row_sum, col_sum = [], [], []

    def after_z(q):
        all_sums(crecv.at[pl.ds(q * 16, 15)], cr.at[q]).wait_recv()
        arriving = jnp.sum(crecv[q * 16 : q * 16 + 16], axis=0)
        scale = jnp.log(arriving * (2.0**-14))
        all_rows(zrecv.at[pl.ds(q * 16, 15)], zr.at[q]).wait_recv()
        high, low = split(zrecv[q * 16 : (q + 1) * 16].reshape(512, 128))
        out = dot_nn(unpack_rows[...], high) + dot_nn(unpack_rows[...], low)
        merged[:, q * 128 : (q + 1) * 128] = out
        weighted.append(out * (jnp.log(out * 0.25) - scale))
        row_sum.append(out)
        col_sum.append(arriving)

    def go(step):
        kind, q = step[0], int(step[1])
        if kind == "p":
            pack(q)
        elif kind == "x":
            after_x(q)
        elif kind == "z":
            after_z(q)
        else:
            after_y(q, "abcd".index(kind))

    for step in ORDER:
        if step == "tags":
            row_tags()
        elif step == "tokens":
            for i in range(4):
                take_token()
                if i < 3:
                    pass_token()
        else:
            go(step)

    tsend[0:1] = jnp.sum(sum(weighted).T, axis=0, keepdims=True)
    tsend[1:2] = jnp.sum(sum(row_sum).T, axis=0, keepdims=True)
    tsend[2:3] = sum(col_sum)
    tsend[3:8] = jnp.zeros((5, 128), F32)
    trecv[0] = tsend[...]

    def t_copy(t):
        return pltpu.make_async_remote_copy(
            src_ref=tsend,
            dst_ref=trecv.at[t],
            send_sem=ts,
            recv_sem=tr,
            device_id=(b, lax.rem(c + t, 8)),
            device_id_type=MESH,
        )

    all_told = pltpu.make_async_remote_copy(
        src_ref=trecv.at[pl.ds(0, 7)],
        dst_ref=trecv.at[pl.ds(0, 7)],
        send_sem=ts,
        recv_sem=tr,
        device_id=(b, lax.rem(c + 1, 8)),
        device_id_type=MESH,
    )
    for t in range(1, 8):
        t_copy(t).start()
    all_columns(xsend.at[pl.ds(0, 3)], xr.at[0]).wait_send()
    all_sends(asend.at[pl.ds(0, 3)], ys.at[0]).wait_send()
    all_sends(bsend.at[pl.ds(0, 3)], ys.at[1]).wait_send()
    all_rows(zsend.at[pl.ds(0, 60)], zr.at[0]).wait_send()
    all_sums(crecv.at[pl.ds(0, 60)], cr.at[0]).wait_send()
    all_told.wait_recv()
    all_told.wait_send()
    everyone = jnp.sum(trecv[...], axis=0)
    out_total = everyone[1:2]
    total = jnp.sum(everyone[2:3], axis=1, keepdims=True)
    terms[...] = (
        everyone[0:1] / out_total
        + jnp.log(total * (2.0**-26))
        - jnp.log(out_total * (2.0**-14))
    )


def shards(counts, merge_map):
    ids = merge_map.reshape(32, 1, 256)
    dma = pltpu.SemaphoreType.DMA
    merged, terms = pl.pallas_call(
        kernel,
        out_shape=(
            jax.ShapeDtypeStruct((128, 512), F32),
            jax.ShapeDtypeStruct((1, 128), F32),
        ),
        in_specs=[
            pl.BlockSpec(memory_space=pltpu.HBM),
            pl.BlockSpec(memory_space=pltpu.HBM),
        ],
        out_specs=(
            pl.BlockSpec(memory_space=pltpu.VMEM),
            pl.BlockSpec(memory_space=pltpu.VMEM),
        ),
        scratch_shapes=[
            pltpu.VMEM((256, 1024), F32),
            pltpu.VMEM((32, 1, 256), I32),
            pltpu.VMEM((2, 256, 1024), BF16),
            pltpu.VMEM((32, 1, 256), I32),
            pltpu.VMEM((NQ, 4, 2, 4, 16, 1), F32),
            pltpu.VMEM((32, 16, 1), F32),
            pltpu.VMEM((128, 512), BF16),
            pltpu.VMEM((512, 256), BF16),
            pltpu.VMEM((NQ, 4, 256, 128), F32),
            pltpu.VMEM((NQ, 4, 256, 128), F32),
            pltpu.VMEM((NQ, 4, 72, 128), F32),
            pltpu.VMEM((NQ, 4, 72, 128), F32),
            pltpu.VMEM((NQ, NP - 1, 4, 64, 128), F32),
            pltpu.VMEM((NQ, NP - 1, 4, 64, 128), F32),
            pltpu.VMEM((NQ * 16, 2, 16, 128), F32),
            pltpu.VMEM((NQ * 16, 2, 16, 128), F32),
            pltpu.VMEM((NQ, 1, 128), F32),
            pltpu.VMEM((NQ * 16, 1, 128), F32),
            pltpu.VMEM((8, 128), F32),
            pltpu.VMEM((8, 8, 128), F32),
            dma,
            dma,
            dma,
            dma((NQ,)),
            dma((2,)),
            dma((NQ, NP)),
            dma,
            dma((NQ,)),
            dma,
            dma((NQ,)),
            dma,
            dma,
            pltpu.SemaphoreType.REGULAR((2,)),
        ],
        compiler_params=pltpu.CompilerParams(
            collective_id=0, has_side_effects=True, vmem_limit_bytes=56_000_000
        ),
    )(counts, ids)
    return merged, terms.reshape(128)


def solution(mesh):
    return jax.shard_map(
        shards,
        mesh=mesh,
        in_specs=(P("blk", "col"), P()),
        out_specs=(P("blk", "col"), P("blk")),
        check_vma=False,
    )
```

time: 58.6 us -> 56.8 us (0.969)
  Pallas kernels: 55.8 us -> 54 us
    pallas_call x1, Pallas kernels: 55.8 us -> 54 us  [shards(): pl.pallas_call(kernel, out_shape=(jax.ShapeDtypeStruct((128, 512), F32),...]
where the time goes in v3:
time: 56.8 us; the launch traced here: 56.6 us
  Pallas kernels  54 us (95%)
  local copies, waits for them, and re-layouts  1.97 us (3%)
  between operations  0.65 us (1%)
    pallas_call x1, Pallas kernels, shards(): pl.pallas_call(kernel, out_shape=(jax.ShapeDtypeStruct((128, 512), F32),...  54 us
    unnamed x4, local copies, waits for them, and re-layouts  1.97 us

profile of v3, /device:TPU:1, one launch (start us, length us, event | category | flops | bytes accessed | tf_op | source)
XLA Modules:
  0.0 56.6 jit_solution(13280448210880083589)
XLA Ops:
  0.6 0.0 copy-start
  0.6 0.7 %copy-done = s32[8192,1]{0,1:T(1,128)S(1)} copy-done((s32[8192,1]{0,1:T(1,128)S(1)}, s32[8192,1]{0,1:T(1,128)}, u32[]{:S(2)}) %copy-start) | copy-done | bytes 32792
  1.4 54.0 %shard_map.41 = (f32[128,512]{1,0:T(8,128)S(1)}, f32[1,128]{1,0:T(1,128)S(1)}) custom-call(f32[256,1024]{1,0:T(8,128)} %counts_hbm.1, s32[32,1,256]{2,1,0:T(1,128)S(1)} %bitcast.2), custom_call_target="tpu_custom_call" | custom-call | tf_op jit(solution)/shard_map/pallas_call | solution.py:438
  55.4 0.7 %copy.6 = f32[128,512]{1,0:T(8,128)} copy(f32[128,512]{1,0:T(8,128)S(1)} %get-tuple-element.8) | data formatting | bytes 524288
  56.1 0.5 copy.7
Async XLA Ops:
  0.6 0.8 %copy-start = (s32[8192,1]{0,1:T(1,128)S(1)}, s32[8192,1]{0,1:T(1,128)}, u32[]{:S(2)}) copy-start(s32[8192,1]{0,1:T(1,128)} %param.3) | copy-start | bytes 98308

commit v4 on v3

--- a/solution.py
+++ b/solution.py
@@ -11,10 +11,11 @@
 I32 = jnp.int32
 NQ = 4
 NP = 4
-Z_STEPS = (4, 3, 5, 0, 2, 6, 1, 7)
+Z_STEPS = (3, 5, 4, 0, 2, 6, 1, 7)
+OWN = 2 * Z_STEPS.index(0)
 ORDER = (
+    "p2",
     "tokens",
-    "p2",
     "x0",
     "p3",
     "tags",
@@ -23,8 +24,8 @@
     "b0",
     "c0",
     "d0",
+    "a1",
     "x2",
-    "a1",
     "b1",
     "c1",
     "d1",
@@ -80,11 +81,10 @@
 
 def kernel(
     counts_hbm,
-    ids_hbm,
+    ids,
     merged,
     terms,
     counts,
-    ids,
     parts,
     keys,
     coltag,
@@ -104,7 +104,6 @@
     tsend,
     trecv,
     in_sem,
-    ids_sem,
     xs,
     xr,
     ys,
@@ -122,8 +121,6 @@
     x, yh = lax.rem(c, 4), lax.div(c, 4)
     core, zz, yl = lax.rem(b, 2), lax.rem(lax.div(b, 2), 8), lax.div(b, 16)
 
-    ids_load = pltpu.make_async_copy(ids_hbm, ids, ids_sem)
-    ids_load.start()
     load = pltpu.make_async_copy(counts_hbm, counts, in_sem)
     load.start()
 
@@ -145,7 +142,6 @@
     for step, k in ((1, 0), (7, 0), (0, 1)):
         greet((z_peer(step, k), c))
 
-    ids_load.wait()
     positions = []
     for g, key in enumerate(slot_keys([ids[c * 4 + g] for g in range(4)])):
         owner = lax.shift_right_logical(key, 4)
@@ -338,7 +334,7 @@
             for i, step in enumerate(Z_STEPS):
                 for k in range(2):
                     if step or k:
-                        at = q * 16 + i * 2 + k - (1 if i * 2 + k > 6 else 0)
+                        at = q * 16 + i * 2 + k - (1 if i * 2 + k > OWN else 0)
                         to_z(step, k, csend.at[q], crecv.at[at], cs, cr.at[q]).start()
         mine = own[0, 0:64] + got[2, 0:64]
         theirs = got[1, 0:64] + got[3, 0:64]
@@ -443,7 +439,7 @@
         ),
         in_specs=[
             pl.BlockSpec(memory_space=pltpu.HBM),
-            pl.BlockSpec(memory_space=pltpu.HBM),
+            pl.BlockSpec(memory_space=pltpu.VMEM),
         ],
         out_specs=(
             pl.BlockSpec(memory_space=pltpu.VMEM),
@@ -451,7 +447,6 @@
         ),
         scratch_shapes=[
             pltpu.VMEM((256, 1024), F32),
-            pltpu.VMEM((32, 1, 256), I32),
             pltpu.VMEM((2, 256, 1024), BF16),
             pltpu.VMEM((32, 1, 256), I32),
             pltpu.VMEM((NQ, 4, 2, 4, 16, 1), F32),
@@ -472,7 +467,6 @@
             pltpu.VMEM((8, 8, 128), F32),
             dma,
             dma,
-            dma,
             dma((NQ,)),
             dma((2,)),
             dma((NQ, NP)),

time: 56.8 us -> 56.2 us (0.989)
  Pallas kernels: 54 us -> 53.4 us
    pallas_call x1, Pallas kernels: 54 us -> 53.4 us  [shards(): pl.pallas_call(kernel, out_shape=(jax.ShapeDtypeStruct((128, 512), F32),...]
where the time goes in v4:
time: 56.2 us; the launch traced here: 56 us
  Pallas kernels  53.4 us (95%)
  local copies, waits for them, and re-layouts  1.97 us (4%)
  between operations  0.65 us (1%)
    pallas_call x1, Pallas kernels, shards(): pl.pallas_call(kernel, out_shape=(jax.ShapeDtypeStruct((128, 512), F32),...  53.4 us
    unnamed x4, local copies, waits for them, and re-layouts  1.97 us

profile of v4, /device:TPU:1, one launch (start us, length us, event | category | flops | bytes accessed | tf_op | source)
XLA Modules:
  0.0 56.0 jit_solution(671722469148495791)
XLA Ops:
  0.6 0.0 copy-start
  0.6 0.7 %copy-done = s32[8192,1]{0,1:T(1,128)S(1)} copy-done((s32[8192,1]{0,1:T(1,128)S(1)}, s32[8192,1]{0,1:T(1,128)}, u32[]{:S(2)}) %copy-start) | copy-done | bytes 32792
  1.4 53.4 %shard_map.41 = (f32[128,512]{1,0:T(8,128)S(1)}, f32[1,128]{1,0:T(1,128)S(1)}) custom-call(f32[256,1024]{1,0:T(8,128)} %counts_hbm.1, s32[32,1,256]{2,1,0:T(1,128)S(1)} %bitcast.2), custom_call_target="tpu_custom_call" | custom-call | tf_op jit(solution)/shard_map/pallas_call | solution.py:434
  54.8 0.7 %copy.6 = f32[128,512]{1,0:T(8,128)} copy(f32[128,512]{1,0:T(8,128)S(1)} %get-tuple-element.8) | data formatting | bytes 524288
  55.5 0.5 copy.7
Async XLA Ops:
  0.6 0.8 %copy-start = (s32[8192,1]{0,1:T(1,128)S(1)}, s32[8192,1]{0,1:T(1,128)}, u32[]{:S(2)}) copy-start(s32[8192,1]{0,1:T(1,128)} %param.3) | copy-start | bytes 98308

commit v5 on v4

--- a/solution.py
+++ b/solution.py
@@ -328,14 +328,6 @@
         y_copy(q, part, 1, 0, few=True).wait_recv()
         own, got = y_refs(q, part)
         to = (q * NP + part) * 4
-        if part == 0:
-            csend[q] = own[0, 64:65] + got[1, 64:65] + got[2, 64:65] + got[3, 64:65]
-            crecv[q * 16 + 15] = csend[q]
-            for i, step in enumerate(Z_STEPS):
-                for k in range(2):
-                    if step or k:
-                        at = q * 16 + i * 2 + k - (1 if i * 2 + k > OWN else 0)
-                        to_z(step, k, csend.at[q], crecv.at[at], cs, cr.at[q]).start()
         mine = own[0, 0:64] + got[2, 0:64]
         theirs = got[1, 0:64] + got[3, 0:64]
         zsend[to : to + 4, 0] = mine.reshape(4, 16, 128)
@@ -348,6 +340,14 @@
                     to_z(step, k, zsend.at[at], zrecv.at[at], zs, zr.at[q]).start()
                 else:
                     zrecv[at] = zsend[at]
+        if part == 0:
+            csend[q] = own[0, 64:65] + got[1, 64:65] + got[2, 64:65] + got[3, 64:65]
+            crecv[q * 16 + 15] = csend[q]
+            for i, step in enumerate(Z_STEPS):
+                for k in range(2):
+                    if step or k:
+                        at = q * 16 + i * 2 + k - (1 if i * 2 + k > OWN else 0)
+                        to_z(step, k, csend.at[q], crecv.at[at], cs, cr.at[q]).start()
 
     weighted, row_sum, col_sum = [], [], []
 
@@ -421,11 +421,12 @@
     everyone = jnp.sum(trecv[...], axis=0)
     out_total = everyone[1:2]
     total = jnp.sum(everyone[2:3], axis=1, keepdims=True)
-    terms[...] = (
+    value = (
         everyone[0:1] / out_total
         + jnp.log(total * (2.0**-26))
         - jnp.log(out_total * (2.0**-14))
     )
+    terms[...] = value.reshape(128)
 
 
 def shards(counts, merge_map):
@@ -435,7 +436,7 @@
         kernel,
         out_shape=(
             jax.ShapeDtypeStruct((128, 512), F32),
-            jax.ShapeDtypeStruct((1, 128), F32),
+            jax.ShapeDtypeStruct((128,), F32),
         ),
         in_specs=[
             pl.BlockSpec(memory_space=pltpu.HBM),
@@ -482,7 +483,7 @@
             collective_id=0, has_side_effects=True, vmem_limit_bytes=56_000_000
         ),
     )(counts, ids)
-    return merged, terms.reshape(128)
+    return merged, terms
 
 
 def solution(mesh):

time: 56.2 us -> 56.1 us (level)
  no operation moved by 1% of the time
where the time goes in v5:
time: 56.1 us; the launch traced here: 55.9 us
  Pallas kernels  53.3 us (95%)
  local copies, waits for them, and re-layouts  1.97 us (4%)
  between operations  0.65 us (1%)
    pallas_call x1, Pallas kernels, shards(): pl.pallas_call(kernel, out_shape=(jax.ShapeDtypeStruct((128, 512), F32),...  53.3 us
    unnamed x4, local copies, waits for them, and re-layouts  1.97 us

profile of v5, /device:TPU:1, one launch (start us, length us, event | category | flops | bytes accessed | tf_op | source)
XLA Modules:
  0.0 55.9 jit_solution(11427348853067090329)
XLA Ops:
  0.6 0.0 copy-start
  0.6 0.7 %copy-done = s32[8192,1]{0,1:T(1,128)S(1)} copy-done((s32[8192,1]{0,1:T(1,128)S(1)}, s32[8192,1]{0,1:T(1,128)}, u32[]{:S(2)}) %copy-start) | copy-done | bytes 32792
  1.4 53.3 %shard_map.41 = (f32[128,512]{1,0:T(8,128)S(1)}, f32[128]{0:T(128)S(1)}) custom-call(f32[256,1024]{1,0:T(8,128)} %counts_hbm.1, s32[32,1,256]{2,1,0:T(1,128)S(1)} %bitcast.1), custom_call_target="tpu_custom_call" | custom-call | tf_op jit(solution)/shard_map/pallas_call | solution.py:435
  54.7 0.7 %copy.6 = f32[128,512]{1,0:T(8,128)} copy(f32[128,512]{1,0:T(8,128)S(1)} %get-tuple-element.4) | data formatting | bytes 524288
  55.4 0.5 copy.7
Async XLA Ops:
  0.6 0.8 %copy-start = (s32[8192,1]{0,1:T(1,128)S(1)}, s32[8192,1]{0,1:T(1,128)}, u32[]{:S(2)}) copy-start(s32[8192,1]{0,1:T(1,128)} %param.3) | copy-start | bytes 98308
